TPU v7x, 32 devices: a whole 2x2x4 slice. The times are simulated.
32 devices in a mesh: row: 4 (over z), col: 8 (over y, x, core).
Axes of the slice: x: 2, y: 2, z: 4, core: 2. Of those that a mesh axis runs over, the one named last changes fastest.
Arguments:
- points: float32 [64, 8192], P(None, ('row', 'col')), may hold values from -10 to 10
- start: float32 [8192], P(('row', 'col')), may hold values from -6 to 6
Outputs:
- basis: float32 [9, 8192], P(None, ('row', 'col'))
- tridiag: float32 [2, 8], replicated
All inputs are finite; a program needn't handle non-finite values.
Results may differ from a plain program's by a relative error of at most 0.028.
Values may be sent and summed in bfloat16 or wider, within the bound.
A program may use at most 64 MiB of HBM per device.

v0:
```python
import functools
import itertools

import jax
import jax.numpy as jnp
from jax import lax
from jax.experimental import pallas as pl
from jax.experimental.pallas import tpu as pltpu
from jax.sharding import PartitionSpec as P

ITERS = 8
LANES = 128


def toggled(index, stride):
    return index + (1 - 2 * (lax.div(index, stride) % 2)) * stride


def masked(index, mask):
    for stride in mask:
        index = toggled(index, stride)
    return index


def subsets(strides):
    return [m for k in range(len(strides) + 1) for m in itertools.combinations(strides, k)]


def split(x):
    hi = x.astype(jnp.bfloat16)
    lo = (x - hi.astype(jnp.float32)).astype(jnp.bfloat16)
    return hi, lo


def body(
    R, C, points, start, basis_out, tri_out,
    gath, vecs, basis, rounded, kmat, lhs, own_sq,
    local_sem, send_sem, z_sem, half_sem, core_sem, vsend_sem, vrecv_sem,
):
    n = R * C
    feats, count = points.shape
    per = count // LANES
    rows = n * per
    half = feats // 2
    scale = 0.5 / feats
    row, col = lax.axis_index("row"), lax.axis_index("col")
    me = row * C + col

    def where(dev):
        return {"row": lax.div(dev, C), "col": lax.rem(dev, C)}

    mine = pltpu.make_async_copy(points, gath.at[me], local_sem.at[0])
    mine.start()
    first = pltpu.make_async_copy(start, vecs.at[ITERS, me], local_sem.at[1])
    first.start()

    barrier = pltpu.get_barrier_semaphore()
    for k in range(1, n):
        pl.semaphore_signal(barrier, inc=1, device_id=where(lax.rem(me + k, n)))
    basis[...] = jnp.zeros_like(basis)
    pl.semaphore_wait(barrier, n - 1)
    mine.wait()
    first.wait()

    def remote(src, dst, recv, dev, send=send_sem):
        return pltpu.make_async_remote_copy(
            src_ref=src, dst_ref=dst, send_sem=send, recv_sem=recv, device_id=where(dev)
        )

    def send_vec(slot):
        for k in range(1, n):
            dev = lax.rem(me + k, n)
            block = vecs.at[slot, me]
            remote(block, block, vrecv_sem.at[slot], dev, vsend_sem.at[slot]).start()

    def wait_vec(slot):
        some = vecs.at[slot, pl.ds(0, n - 1)]
        pltpu.make_async_copy(some, some, vrecv_sem.at[slot]).wait()

    def wait_vec_sent(slot):
        some = vecs.at[slot, pl.ds(0, n - 1)]
        pltpu.make_async_copy(some, some, vsend_sem.at[slot]).wait()

    for k in range(1, R):
        dev = lax.rem(row + k, R) * C + col
        remote(gath.at[me], gath.at[me], z_sem.at[row], dev).start()

    strides = []
    s = 2
    while s < C:
        strides.append(s)
        s *= 2
    orders = (strides, strides[::-1])

    def half_copy(order, h, stage, i, mask, r, to):
        block = gath.at[r * C + masked(col, mask), pl.ds(h * half, half)]
        return remote(block, block, half_sem.at[h, 2**stage - 1 + i, r], row * C + toggled(col, order[stage])) if to else block

    def start_stage(stage, r):
        for h, order in enumerate(orders):
            for i, mask in enumerate(subsets(order[:stage])):
                half_copy(order, h, stage, i, mask, r, True).start()

    def wait_stage(stage, r):
        for h, order in enumerate(orders):
            for i, mask in enumerate(subsets(order[:stage])):
                block = gath.at[r * C + masked(toggled(col, order[stage]), mask), pl.ds(h * half, half)]
                pltpu.make_async_copy(block, block, half_sem.at[h, 2**stage - 1 + i, r]).wait()

    combos = subsets(strides)

    def start_core(r):
        for i, mask in enumerate(combos):
            block = gath.at[r * C + masked(col, mask)]
            remote(block, block, core_sem.at[i, r], row * C + toggled(col, 1)).start()

    def wait_core(r):
        for i, mask in enumerate(combos):
            block = gath.at[r * C + masked(toggled(col, 1), mask)]
            pltpu.make_async_copy(block, block, core_sem.at[i, r]).wait()

    def group(k):
        return lax.rem(row + k, R)

    start_stage(0, row)
    send_vec(ITERS)

    own = gath[me]
    hi, lo = split(own)
    lhs[...] = jnp.concatenate([hi, hi, lo], axis=0).astype(jnp.float32).T.astype(jnp.bfloat16)
    full = hi.astype(jnp.float32) + lo.astype(jnp.float32)
    own_sq[...] = jnp.broadcast_to(jnp.sum((full * full).T, axis=1, keepdims=True), own_sq.shape)

    def make_block(dev):
        hi, lo = split(gath[dev])
        x = hi.astype(jnp.float32) + lo.astype(jnp.float32)
        sq = jnp.sum(x * x, axis=0, keepdims=True)
        rhs = jnp.concatenate([hi, lo, hi], axis=0)
        cross = jnp.dot(lhs[...], rhs, preferred_element_type=jnp.float32)
        for p in range(per):
            cut = slice(p * LANES, (p + 1) * LANES)
            dist = own_sq[...] + sq[:, cut] - 2.0 * cross[:, cut]
            kmat[dev * per + p] = jnp.exp(-dist * scale).astype(jnp.bfloat16).astype(jnp.float32)

    def make_group(r, c):
        for mask in combos:
            make_block(r * C + masked(c, mask))

    def loop(lo, hi, f):
        lax.fori_loop(lo, hi, lambda k, x: (f(k), x)[1], 0)

    def z_step(k):
        r = group(k)
        block = gath.at[r * C + col]
        pltpu.make_async_copy(block, block, z_sem.at[r]).wait()
        start_stage(0, r)

    loop(1, R, z_step)
    for stage in range(1, len(strides)):
        def mid(k, stage=stage):
            wait_stage(stage - 1, group(k))
            start_stage(stage, group(k))
        loop(0, R, mid)

    def last(k):
        wait_stage(len(strides) - 1, group(k))
        start_core(group(k))
    loop(0, R, last)
    loop(0, R, lambda k: make_group(group(k), col))

    def final(k):
        wait_core(group(k))
        make_group(group(k), toggled(col, 1))
    loop(0, R, final)

    pltpu.make_async_copy(gath.at[pl.ds(0, n - 1)], gath.at[pl.ds(0, n - 1)], send_sem).wait()

    def total(x):
        return jnp.sum(x, keepdims=True)

    wait_vec(ITERS)
    wait_vec_sent(ITERS)
    s = vecs[ITERS].reshape(rows, LANES)

    def keep(j, q):
        basis[j] = q
        rounded[...] = q.astype(jnp.bfloat16).astype(jnp.float32)

    keep(0, s / jnp.sqrt(total(s * s) + 1e-06))

    lane = lax.broadcasted_iota(jnp.int32, (2, LANES), 1)
    sub = lax.broadcasted_iota(jnp.int32, (2, LANES), 0)

    def step(j, tri):
        def chunk(c, acc):
            return acc + kmat[c] * rounded[pl.ds(c, 1), :]

        acc = lax.fori_loop(0, rows, chunk, jnp.zeros((count, LANES), jnp.float32), unroll=4)
        mine = jnp.sum(acc.T, axis=0, keepdims=True)
        for p in range(per):
            vecs[j, me, p : p + 1, :] = mine[:, p * LANES : (p + 1) * LANES]
        send_vec(j)
        wait_vec(j)
        wait_vec_sent(j)
        w = vecs[j].reshape(rows, LANES)
        h1 = [total(basis[i] * w) for i in range(ITERS)]
        for i in range(ITERS):
            w = w - h1[i] * basis[i]
        h2 = [total(basis[i] * w) for i in range(ITERS)]
        for i in range(ITERS):
            w = w - h2[i] * basis[i]
        beta = jnp.sqrt(total(w * w) + 1e-06)
        keep(j + 1, w / beta)
        alpha = sum(jnp.where(j == i, h, 0.0) for i, h in enumerate(h1))
        return jnp.where(lane == j, jnp.where(sub == 0, alpha, beta), tri)

    tri = lax.fori_loop(0, ITERS, step, jnp.zeros((2, LANES), jnp.float32))
    tri_out[...] = tri[:, :ITERS]
    basis_out[...] = basis[:, pl.ds(me * per, per), :]


def per_device(R, C, points, start):
    feats, count = points.shape
    n = R * C
    per = count // LANES
    rows = n * per
    vmem = pl.BlockSpec(memory_space=pltpu.VMEM)
    anywhere = pl.BlockSpec(memory_space=pl.ANY)
    basis, tri = pl.pallas_call(
        functools.partial(body, R, C),
        out_shape=(
            jax.ShapeDtypeStruct((ITERS + 1, per, LANES), jnp.float32),
            jax.ShapeDtypeStruct((2, ITERS), jnp.float32),
        ),
        in_specs=[anywhere, anywhere],
        out_specs=(vmem, vmem),
        scratch_shapes=[
            pltpu.VMEM((n, feats, count), jnp.float32),
            pltpu.VMEM((ITERS + 1, n, per, LANES), jnp.float32),
            pltpu.VMEM((ITERS + 1, rows, LANES), jnp.float32),
            pltpu.VMEM((rows, LANES), jnp.float32),
            pltpu.VMEM((rows, count, LANES), jnp.float32),
            pltpu.VMEM((count, 3 * feats), jnp.bfloat16),
            pltpu.VMEM((count, LANES), jnp.float32),
            pltpu.SemaphoreType.DMA((2,)),
            pltpu.SemaphoreType.DMA,
            pltpu.SemaphoreType.DMA((R,)),
            pltpu.SemaphoreType.DMA((2, C // 2 - 1, R)),
            pltpu.SemaphoreType.DMA((C // 2, R)),
            pltpu.SemaphoreType.DMA((ITERS + 1,)),
            pltpu.SemaphoreType.DMA((ITERS + 1,)),
        ],
        compiler_params=pltpu.CompilerParams(
            collective_id=0, has_side_effects=True, vmem_limit_bytes=60 * 1024 * 1024
        ),
    )(points, start.reshape(per, LANES))
    return basis.reshape(ITERS + 1, count), tri


def solution(mesh):
    R, C = mesh.shape["row"], mesh.shape["col"]
    return jax.shard_map(
        functools.partial(per_device, R, C),
        mesh=mesh,
        in_specs=(P(None, ("row", "col")), P(("row", "col"))),
        out_specs=(P(None, ("row", "col")), P()),
        check_vma=False,
    )
```

profile of v0, /device:TPU:0, one launch (start us, length us, event | category | flops | bytes accessed | tf_op | source)
XLA Modules:
  0.0 79.8 jit_solution(6506156286005656247)
XLA Ops:
  0.6 76.6 %shard_map.41 = (f32[9,2,128]{2,1,0:T(2,128)}, f32[2,8]{1,0:T(2,128)}) custom-call(f32[64,256]{1,0:T(8,128)} %points.1, f32[2,128]{1,0:T(2,128)} %bitcast.6), custom_call_target="tpu_custom_call" | custom-call | tf_op jit(solution)/shard_map/pallas_call | solution.py:229
  77.3 0.7 pad
  78.0 0.6 copy.4
  78.6 0.0 copy-start
  78.6 0.7 copy-done
  79.3 0.6 copy.6
Async XLA Ops:
  78.6 0.7 copy-start
where the time goes:
time: 80.1 us; the launch traced here: 79.8 us
  Pallas kernels  76.6 us (96%)
  local copies, waits for them, and re-layouts  2.54 us (3%)
    pallas_call x1, Pallas kernels, per_device(): pl.pallas_call(functools.partial(body, R, C), out_shape=(jax.ShapeDtypeSt...  76.6 us
    unnamed x5, local copies, waits for them, and re-layouts  2.54 us

commit v1 on v0

--- a/solution.py
+++ b/solution.py
@@ -33,7 +33,7 @@
 
 
 def body(
-    R, C, points, start, basis_out, tri_out,
+    R, C, points, start, out,
     gath, vecs, basis, rounded, kmat, lhs, own_sq,
     local_sem, send_sem, z_sem, half_sem, core_sem, vsend_sem, vrecv_sem,
 ):
@@ -51,7 +51,7 @@
 
     mine = pltpu.make_async_copy(points, gath.at[me], local_sem.at[0])
     mine.start()
-    first = pltpu.make_async_copy(start, vecs.at[ITERS, me], local_sem.at[1])
+    first = pltpu.make_async_copy(start, vecs.at[ITERS, pl.ds(pl.multiple_of(me * per, per), per)], local_sem.at[1])
     first.start()
 
     barrier = pltpu.get_barrier_semaphore()
@@ -70,19 +70,22 @@
     def send_vec(slot):
         for k in range(1, n):
             dev = lax.rem(me + k, n)
-            block = vecs.at[slot, me]
+            block = vecs.at[slot, pl.ds(pl.multiple_of(me * per, per), per)]
             remote(block, block, vrecv_sem.at[slot], dev, vsend_sem.at[slot]).start()
 
     def wait_vec(slot):
-        some = vecs.at[slot, pl.ds(0, n - 1)]
+        some = vecs.at[slot, pl.ds(0, rows - per)]
         pltpu.make_async_copy(some, some, vrecv_sem.at[slot]).wait()
 
     def wait_vec_sent(slot):
-        some = vecs.at[slot, pl.ds(0, n - 1)]
+        some = vecs.at[slot, pl.ds(0, rows - per)]
         pltpu.make_async_copy(some, some, vsend_sem.at[slot]).wait()
 
+    def group(k):
+        return masked(row, [1 << t for t in range(k.bit_length()) if k >> t & 1])
+
     for k in range(1, R):
-        dev = lax.rem(row + k, R) * C + col
+        dev = group(k) * C + col
         remote(gath.at[me], gath.at[me], z_sem.at[row], dev).start()
 
     strides = []
@@ -118,9 +121,6 @@
         for i, mask in enumerate(combos):
             block = gath.at[r * C + masked(toggled(col, 1), mask)]
             pltpu.make_async_copy(block, block, core_sem.at[i, r]).wait()
-
-    def group(k):
-        return lax.rem(row + k, R)
 
     start_stage(0, row)
     send_vec(ITERS)
@@ -146,41 +146,37 @@
         for mask in combos:
             make_block(r * C + masked(c, mask))
 
-    def loop(lo, hi, f):
-        lax.fori_loop(lo, hi, lambda k, x: (f(k), x)[1], 0)
-
-    def z_step(k):
-        r = group(k)
-        block = gath.at[r * C + col]
-        pltpu.make_async_copy(block, block, z_sem.at[r]).wait()
-        start_stage(0, r)
-
-    loop(1, R, z_step)
-    for stage in range(1, len(strides)):
-        def mid(k, stage=stage):
-            wait_stage(stage - 1, group(k))
-            start_stage(stage, group(k))
-        loop(0, R, mid)
-
-    def last(k):
-        wait_stage(len(strides) - 1, group(k))
-        start_core(group(k))
-    loop(0, R, last)
-    loop(0, R, lambda k: make_group(group(k), col))
-
-    def final(k):
-        wait_core(group(k))
-        make_group(group(k), toggled(col, 1))
-    loop(0, R, final)
+    depth = len(strides)
+    for t in range(R + depth + 1):
+        if 0 < t < R:
+            block = gath.at[group(t) * C + col]
+            pltpu.make_async_copy(block, block, z_sem.at[group(t)]).wait()
+            start_stage(0, group(t))
+        for stage in range(1, depth):
+            if 0 <= t - stage < R:
+                wait_stage(stage - 1, group(t - stage))
+                start_stage(stage, group(t - stage))
+        if 0 <= t - depth < R:
+            wait_stage(depth - 1, group(t - depth))
+            start_core(group(t - depth))
+            make_group(group(t - depth), col)
+        if 0 <= t - depth - 1 < R:
+            wait_core(group(t - depth - 1))
+            make_group(group(t - depth - 1), toggled(col, 1))
 
     pltpu.make_async_copy(gath.at[pl.ds(0, n - 1)], gath.at[pl.ds(0, n - 1)], send_sem).wait()
+
+    def dots(w):
+        parts = [jnp.sum((basis[i] * w).reshape(rows // 8, 8, LANES), axis=0) for i in range(ITERS)]
+        cols = jnp.sum(jnp.concatenate([jnp.sum(x, axis=0, keepdims=True) for x in parts], axis=0), axis=1, keepdims=True)
+        return [cols[i : i + 1] for i in range(ITERS)]
 
     def total(x):
         return jnp.sum(x, keepdims=True)
 
     wait_vec(ITERS)
     wait_vec_sent(ITERS)
-    s = vecs[ITERS].reshape(rows, LANES)
+    s = vecs[ITERS]
 
     def keep(j, q):
         basis[j] = q
@@ -195,18 +191,18 @@
         def chunk(c, acc):
             return acc + kmat[c] * rounded[pl.ds(c, 1), :]
 
-        acc = lax.fori_loop(0, rows, chunk, jnp.zeros((count, LANES), jnp.float32), unroll=4)
+        acc = lax.fori_loop(0, rows, chunk, jnp.zeros((count, LANES), jnp.float32), unroll=16)
         mine = jnp.sum(acc.T, axis=0, keepdims=True)
         for p in range(per):
-            vecs[j, me, p : p + 1, :] = mine[:, p * LANES : (p + 1) * LANES]
+            vecs[j, pl.ds(me * per + p, 1), :] = mine[:, p * LANES : (p + 1) * LANES]
         send_vec(j)
         wait_vec(j)
         wait_vec_sent(j)
-        w = vecs[j].reshape(rows, LANES)
-        h1 = [total(basis[i] * w) for i in range(ITERS)]
+        w = vecs[j]
+        h1 = dots(w)
         for i in range(ITERS):
             w = w - h1[i] * basis[i]
-        h2 = [total(basis[i] * w) for i in range(ITERS)]
+        h2 = dots(w)
         for i in range(ITERS):
             w = w - h2[i] * basis[i]
         beta = jnp.sqrt(total(w * w) + 1e-06)
@@ -215,8 +211,11 @@
         return jnp.where(lane == j, jnp.where(sub == 0, alpha, beta), tri)
 
     tri = lax.fori_loop(0, ITERS, step, jnp.zeros((2, LANES), jnp.float32))
-    tri_out[...] = tri[:, :ITERS]
-    basis_out[...] = basis[:, pl.ds(me * per, per), :]
+    for p in range(per):
+        cut = slice(p * LANES, (p + 1) * LANES)
+        for j in range(ITERS + 1):
+            out[j : j + 1, cut] = basis[j, pl.ds(me * per + p, 1), :]
+    out[ITERS + 1 : ITERS + 3, :LANES] = tri
 
 
 def per_device(R, C, points, start):
@@ -226,17 +225,14 @@
     rows = n * per
     vmem = pl.BlockSpec(memory_space=pltpu.VMEM)
     anywhere = pl.BlockSpec(memory_space=pl.ANY)
-    basis, tri = pl.pallas_call(
+    out = pl.pallas_call(
         functools.partial(body, R, C),
-        out_shape=(
-            jax.ShapeDtypeStruct((ITERS + 1, per, LANES), jnp.float32),
-            jax.ShapeDtypeStruct((2, ITERS), jnp.float32),
-        ),
+        out_shape=jax.ShapeDtypeStruct((ITERS + 3, count), jnp.float32),
         in_specs=[anywhere, anywhere],
-        out_specs=(vmem, vmem),
+        out_specs=vmem,
         scratch_shapes=[
             pltpu.VMEM((n, feats, count), jnp.float32),
-            pltpu.VMEM((ITERS + 1, n, per, LANES), jnp.float32),
+            pltpu.VMEM((ITERS + 1, rows, LANES), jnp.float32),
             pltpu.VMEM((ITERS + 1, rows, LANES), jnp.float32),
             pltpu.VMEM((rows, LANES), jnp.float32),
             pltpu.VMEM((rows, count, LANES), jnp.float32),
@@ -254,7 +250,7 @@
             collective_id=0, has_side_effects=True, vmem_limit_bytes=60 * 1024 * 1024
         ),
     )(points, start.reshape(per, LANES))
-    return basis.reshape(ITERS + 1, count), tri
+    return out[: ITERS + 1], out[ITERS + 1 :, :ITERS]
 
 
 def solution(mesh):

time: 80.1 us -> 74.6 us (0.931)
  Pallas kernels: 76.6 us -> 71.1 us
    pallas_call x1, Pallas kernels: 76.6 us -> 71.1 us  [per_device(): pl.pallas_call(functools.partial(body, R, C), out_shape=jax.ShapeDtypeStr...]
    slice x0 -> x1, local copies, waits for them, and re-layouts: none -> 1.24 us  [per_device(): return (out[:ITERS + 1], out[ITERS + 1:, :ITERS])]
    unnamed x5 -> x1, local copies, waits for them, and re-layouts: 2.54 us -> 1.32 us
where the time goes in v1:
time: 74.6 us; the launch traced here: 74.3 us
  Pallas kernels  71.1 us (95%)
  local copies, waits for them, and re-layouts  2.56 us (3%)
    pallas_call x1, Pallas kernels, per_device(): pl.pallas_call(functools.partial(body, R, C), out_shape=jax.ShapeDtypeStr...  71.1 us

profile of v1, /device:TPU:0, one launch (start us, length us, event | category | flops | bytes accessed | tf_op | source)
XLA Modules:
  0.0 74.3 jit_solution(12222579814310854882)
XLA Ops:
  0.6 71.1 %shard_map.41 = f32[11,256]{1,0:T(8,128)} custom-call(f32[64,256]{1,0:T(8,128)} %points.1, f32[2,128]{1,0:T(2,128)} %bitcast.3), custom_call_target="tpu_custom_call" | custom-call | tf_op jit(solution)/shard_map/pallas_call | solution.py:228
  71.7 1.2 %slice.7 = f32[2,8]{1,0:T(2,128)} slice(f32[11,256]{1,0:T(8,128)} %shard_map.41), slice={[9:11], [0:8]} | slice | bytes 128 | tf_op jit(solution)/shard_map/slice | solution.py:253
  72.9 1.3 %copy.5 = f32[9,256]{1,0:T(8,128)} copy(f32[9,256]{1,0:T(8,128)} %bitcast.2) | data formatting | bytes 18432

commit v2 on v1

--- a/solution.py
+++ b/solution.py
@@ -67,11 +67,23 @@
             src_ref=src, dst_ref=dst, send_sem=send, recv_sem=recv, device_id=where(dev)
         )
 
+    def xor(index, mask):
+        return masked(index, [1 << t for t in range(mask.bit_length()) if mask >> t & 1])
+
+    row_of = [xor(row, k) for k in range(R)]
+    col_of = [xor(col, k) for k in range(C)]
+    far_first = sorted(range(1, n), key=lambda k: (-(k // C), -(k % C).bit_count()))
+
     def send_vec(slot):
-        for k in range(1, n):
-            dev = lax.rem(me + k, n)
-            block = vecs.at[slot, pl.ds(pl.multiple_of(me * per, per), per)]
-            remote(block, block, vrecv_sem.at[slot], dev, vsend_sem.at[slot]).start()
+        block = vecs.at[slot, pl.ds(pl.multiple_of(me * per, per), per)]
+        for k in far_first:
+            pltpu.make_async_remote_copy(
+                src_ref=block,
+                dst_ref=block,
+                send_sem=vsend_sem.at[slot],
+                recv_sem=vrecv_sem.at[slot],
+                device_id={"row": row_of[k // C], "col": col_of[k % C]},
+            ).start()
 
     def wait_vec(slot):
         some = vecs.at[slot, pl.ds(0, rows - per)]
@@ -175,7 +187,6 @@
         return jnp.sum(x, keepdims=True)
 
     wait_vec(ITERS)
-    wait_vec_sent(ITERS)
     s = vecs[ITERS]
 
     def keep(j, q):
@@ -191,13 +202,14 @@
         def chunk(c, acc):
             return acc + kmat[c] * rounded[pl.ds(c, 1), :]
 
-        acc = lax.fori_loop(0, rows, chunk, jnp.zeros((count, LANES), jnp.float32), unroll=16)
-        mine = jnp.sum(acc.T, axis=0, keepdims=True)
         for p in range(per):
-            vecs[j, pl.ds(me * per + p, 1), :] = mine[:, p * LANES : (p + 1) * LANES]
+            def chunk(c, acc, p=p):
+                return acc + kmat[c, p * LANES : (p + 1) * LANES] * rounded[pl.ds(c, 1), :]
+
+            acc = lax.fori_loop(0, rows, chunk, jnp.zeros((LANES, LANES), jnp.float32), unroll=32)
+            vecs[j, pl.ds(me * per + p, 1), :] = jnp.sum(acc.T, axis=0, keepdims=True)
         send_vec(j)
         wait_vec(j)
-        wait_vec_sent(j)
         w = vecs[j]
         h1 = dots(w)
         for i in range(ITERS):
@@ -216,6 +228,7 @@
         for j in range(ITERS + 1):
             out[j : j + 1, cut] = basis[j, pl.ds(me * per + p, 1), :]
     out[ITERS + 1 : ITERS + 3, :LANES] = tri
+    lax.fori_loop(0, ITERS + 1, lambda j, x: (wait_vec_sent(j), x)[1], 0)
 
 
 def per_device(R, C, points, start):

time: 74.6 us -> 73.4 us (0.984)
  Pallas kernels: 71.1 us -> 69.9 us
    pallas_call x1, Pallas kernels: 71.1 us -> 69.9 us  [per_device(): pl.pallas_call(functools.partial(body, R, C), out_shape=jax.ShapeDtypeStr...]
where the time goes in v2:
time: 73.4 us; the launch traced here: 73.1 us
  Pallas kernels  69.9 us (95%)
  local copies, waits for them, and re-layouts  2.56 us (3%)
    pallas_call x1, Pallas kernels, per_device(): pl.pallas_call(functools.partial(body, R, C), out_shape=jax.ShapeDtypeStr...  69.9 us

profile of v2, /device:TPU:0, one launch (start us, length us, event | category | flops | bytes accessed | tf_op | source)
XLA Modules:
  0.0 73.1 jit_solution(13366516782966580038)
XLA Ops:
  0.6 69.9 %shard_map.41 = f32[11,256]{1,0:T(8,128)} custom-call(f32[64,256]{1,0:T(8,128)} %points.1, f32[2,128]{1,0:T(2,128)} %bitcast.3), custom_call_target="tpu_custom_call" | custom-call | tf_op jit(solution)/shard_map/pallas_call | solution.py:241
  70.5 1.2 %slice.7 = f32[2,8]{1,0:T(2,128)} slice(f32[11,256]{1,0:T(8,128)} %shard_map.41), slice={[9:11], [0:8]} | slice | bytes 128 | tf_op jit(solution)/shard_map/slice | solution.py:266
  71.7 1.3 %copy.5 = f32[9,256]{1,0:T(8,128)} copy(f32[9,256]{1,0:T(8,128)} %bitcast.2) | data formatting | bytes 18432
